TPU v7x, 512 devices: a whole 4x4x16 slice. The times are simulated.
512 devices in a mesh: gx: 16 (over y_lo, x, core), gy: 32 (over y_hi, z).
Axes of the slice: x: 4, y: 4 (y_hi: 2, y_lo: 2; y = y_hi * 2 + y_lo), z: 16, core: 2. Of those that a mesh axis runs over, the one named last changes fastest.
Arguments:
- sources: float32 [32, 16, 256, 1024], P('gy', 'gx'), may hold values from -6 to 6
- coeff_in: bfloat16 [32, 16, 256, 256], P('gy', 'gx'), may hold values from -0.375 to 0.375
- transfer: bfloat16 [8, 32, 16, 256, 512], P(None, 'gy', 'gx'), may hold values from -0.25 to 0.25
- coeff_out: bfloat16 [32, 16, 256, 256], P('gy', 'gx'), may hold values from -0.375 to 0.375
Outputs:
- targets: float32 [32, 16, 256, 1024], P('gy', 'gx')
All inputs are finite; a program needn't handle non-finite values.
Results may differ from a plain program's by a relative error of at most 0.015.
Values may be sent and summed in bfloat16 or wider, within the bound.
No kernel may reach another device: no remote copies, remote signals or barrier semaphores. Data moves between devices by JAX's collectives and lax.ppermute only.
A program may use at most 64 MiB of HBM per device.

v0:
```python
import jax
import jax.numpy as jnp
from jax import lax
from jax.sharding import PartitionSpec as P

LEVELS = 8


def swapped(value, axis, bit):
    mask = 2**bit
    pairs = [(source, source ^ mask) for source in range(lax.axis_size(axis))]
    return lax.ppermute(value, axis, pairs)


def combine(own, other, weights, upper):
    rank_rows = own.shape[0]
    lower_part = jnp.where(upper, other, own)
    upper_part = jnp.where(upper, own, other)
    total = jnp.dot(weights[:, :rank_rows], lower_part, preferred_element_type=jnp.float32)
    total = total + jnp.dot(weights[:, rank_rows:], upper_part, preferred_element_type=jnp.float32)
    return total.astype(jnp.bfloat16)


def partner_half(state, level_bit, low_bits):
    if level_bit < low_bits:
        return swapped(state, "gx", level_bit)
    return swapped(state, "gy", level_bit - low_bits)


def body(sources, coeff_in, transfer, coeff_out):
    low_bits = lax.axis_size("gx").bit_length() - 1
    nbits = low_bits + lax.axis_size("gy").bit_length() - 1
    position = lax.axis_index("gy") * lax.axis_size("gx") + lax.axis_index("gx")
    source_block = sources[0, 0].astype(jnp.bfloat16)
    state = jnp.dot(coeff_in[0, 0], source_block, preferred_element_type=jnp.float32).astype(
        jnp.bfloat16
    )
    cols_count = state.shape[1]
    for level in range(LEVELS):
        level_bit = nbits - 1 - level % nbits
        upper = position >> level_bit & 1 == 1
        weights = transfer[level, 0, 0]
        middle = cols_count // 2
        first_half = state[:, :middle]
        second_half = state[:, middle:]
        other_first = partner_half(first_half, level_bit, low_bits)
        new_first = combine(first_half, other_first, weights, upper)
        other_second = partner_half(second_half, level_bit, low_bits)
        new_second = combine(second_half, other_second, weights, upper)
        state = jnp.concatenate([new_first, new_second], axis=1)
    result = jnp.dot(coeff_out[0, 0], state, preferred_element_type=jnp.float32)
    return result[None, None]


def solution(mesh):
    placed = (
        P("gy", "gx", None, None),
        P("gy", "gx", None, None),
        P(None, "gy", "gx", None, None),
        P("gy", "gx", None, None),
    )
    return jax.shard_map(
        body, mesh=mesh, in_specs=placed, out_specs=P("gy", "gx", None, None), check_vma=False
    )
```

profile of v0, /device:TPU:2, one launch (start us, length us, event | category | flops | bytes accessed | tf_op | source)
XLA Modules:
  0.0 195.4 jit_solution(10660584500510336189)
XLA Ops:
  0.0 0.9 copy-done
  0.9 1.5 convolution_convert_fusion
  3.2 5.1 %collective-permute-start = (bf16[256,512]{1,0:T(8,128)(2,1)S(1)}, bf16[256,512]{1,0:T(8,128)(2,1)S(1)}, u32[]{:S(2)}, u32[]{:S(2)}) collective-permute-start(bf16[256,512]{1,0:T(8,128)(2,1)S(1)} %get-tuple-element.13), channel_id=1, source_target_pairs={{0,16},{1,17},{2,18},{3,19},{4,20},{5,21},{6,22},{7,23},{8,24},{9,... | collective-permute-start | bytes 786440 | tf_op jit(solution)/shard_map/ppermute | solution.py:12
  8.3 2.2 %collective-permute-start.8 = (bf16[256,512]{1,0:T(8,128)(2,1)}, bf16[256,512]{1,0:T(8,128)(2,1)S(1)}, u32[]{:S(2)}, u32[]{:S(2)}) collective-permute-start(bf16[256,512]{1,0:T(8,128)(2,1)} %get-tuple-element.14), channel_id=1, source_target_pairs={{0,16},{1,17},{2,18},{3,19},{4,20},{5,21},{6,22},{7,23},{8,24},{9,... | collective-permute-start | bytes 786440 | tf_op jit(solution)/shard_map/ppermute | solution.py:12
  10.7 9.5 %collective-permute-done.8 = bf16[256,512]{1,0:T(8,128)(2,1)S(1)} collective-permute-done((bf16[256,512]{1,0:T(8,128)(2,1)}, bf16[256,512]{1,0:T(8,128)(2,1)S(1)}, u32[]{:S(2)}, u32[]{:S(2)}) %collective-permute-start.8) | collective-permute-done | bytes 262176 | tf_op jit(solution)/shard_map/ppermute | solution.py:12
  20.8 15.7 %collective-permute-start.9 = (bf16[256,512]{0,1:T(8,128)(2,1)S(1)}, bf16[256,512]{0,1:T(8,128)(2,1)S(1)}, u32[]{:S(2)}, u32[]{:S(2)}) collective-permute-start(bf16[256,512]{0,1:T(8,128)(2,1)S(1)} %fusion.23), channel_id=1, source_target_pairs={{0,8},{1,9},{2,10},{3,11},{4,12},{5,13},{6,14},{7,15},{8,0},{9,1},... | collective-permute-start | bytes 786440 | tf_op jit(solution)/shard_map/ppermute | solution.py:12
  37.1 1.9 collective-permute-start.1
  39.1 11.2 %collective-permute-done.9 = bf16[256,512]{0,1:T(8,128)(2,1)S(1)} collective-permute-done((bf16[256,512]{0,1:T(8,128)(2,1)S(1)}, bf16[256,512]{0,1:T(8,128)(2,1)S(1)}, u32[]{:S(2)}, u32[]{:S(2)}) %collective-permute-start.9) | collective-permute-done | bytes 262176 | tf_op jit(solution)/shard_map/ppermute | solution.py:12
  50.8 23.2 %collective-permute-start.10 = (bf16[256,512]{0,1:T(8,128)(2,1)S(1)}, bf16[256,512]{0,1:T(8,128)(2,1)S(1)}, u32[]{:S(2)}, u32[]{:S(2)}) collective-permute-start(bf16[256,512]{0,1:T(8,128)(2,1)S(1)} %fusion.22), channel_id=1, source_target_pairs={{0,4},{1,5},{2,6},{3,7},{4,0},{5,1},{6,2},{7,3},{8,12},{9,13},{10,... | collective-permute-start | bytes 786440 | tf_op jit(solution)/shard_map/ppermute | solution.py:12
  74.6 9.9 %collective-permute-start.2 = (bf16[256,512]{0,1:T(8,128)(2,1)S(1)}, bf16[256,512]{0,1:T(8,128)(2,1)S(1)}, u32[]{:S(2)}, u32[]{:S(2)}) collective-permute-start(bf16[256,512]{0,1:T(8,128)(2,1)S(1)} %fusion.30), channel_id=1, source_target_pairs={{0,4},{1,5},{2,6},{3,7},{4,0},{5,1},{6,2},{7,3},{8,12},{9,13},{10,... | collective-permute-start | bytes 786440 | tf_op jit(solution)/shard_map/ppermute | solution.py:12
  84.5 37.1 %collective-permute-done.10 = bf16[256,512]{0,1:T(8,128)(2,1)S(1)} collective-permute-done((bf16[256,512]{0,1:T(8,128)(2,1)S(1)}, bf16[256,512]{0,1:T(8,128)(2,1)S(1)}, u32[]{:S(2)}, u32[]{:S(2)}) %collective-permute-start.10) | collective-permute-done | bytes 262176 | tf_op jit(solution)/shard_map/ppermute | solution.py:12
  122.1 1.9 collective-permute-start.11
  124.1 3.2 %collective-permute-done.2 = bf16[256,512]{0,1:T(8,128)(2,1)S(1)} collective-permute-done((bf16[256,512]{0,1:T(8,128)(2,1)S(1)}, bf16[256,512]{0,1:T(8,128)(2,1)S(1)}, u32[]{:S(2)}, u32[]{:S(2)}) %collective-permute-start.2) | collective-permute-done | bytes 262176 | tf_op jit(solution)/shard_map/ppermute | solution.py:12
  127.7 1.9 collective-permute-start.3
  129.7 14.4 %collective-permute-done.11 = bf16[256,512]{0,1:T(8,128)(2,1)S(1)} collective-permute-done((bf16[256,512]{0,1:T(8,128)(2,1)S(1)}, bf16[256,512]{0,1:T(8,128)(2,1)S(1)}, u32[]{:S(2)}, u32[]{:S(2)}) %collective-permute-start.11) | collective-permute-done | bytes 262176 | tf_op jit(solution)/shard_map/ppermute | solution.py:12
  144.6 1.9 collective-permute-start.12
  146.5 3.1 %collective-permute-done.3 = bf16[256,512]{0,1:T(8,128)(2,1)S(1)} collective-permute-done((bf16[256,512]{0,1:T(8,128)(2,1)S(1)}, bf16[256,512]{0,1:T(8,128)(2,1)S(1)}, u32[]{:S(2)}, u32[]{:S(2)}) %collective-permute-start.3) | collective-permute-done | bytes 262176 | tf_op jit(solution)/shard_map/ppermute | solution.py:12
  150.2 1.9 collective-permute-start.4
  152.1 3.6 %collective-permute-done.12 = bf16[256,512]{0,1:T(8,128)(2,1)S(1)} collective-permute-done((bf16[256,512]{0,1:T(8,128)(2,1)S(1)}, bf16[256,512]{0,1:T(8,128)(2,1)S(1)}, u32[]{:S(2)}, u32[]{:S(2)}) %collective-permute-start.12) | collective-permute-done | bytes 262176 | tf_op jit(solution)/shard_map/ppermute | solution.py:12
  156.2 3.2 %collective-permute-start.13 = (bf16[256,512]{0,1:T(8,128)(2,1)S(1)}, bf16[256,512]{0,1:T(8,128)(2,1)S(1)}, u32[]{:S(2)}, u32[]{:S(2)}) collective-permute-start(bf16[256,512]{0,1:T(8,128)(2,1)S(1)} %fusion.19), channel_id=1, source_target_pairs={{0,256},{32,288},{64,320},{96,352},{128,384},{160,416},{192,448},{... | collective-permute-start | bytes 786440 | tf_op jit(solution)/shard_map/ppermute | solution.py:12
  159.4 1.5 collective-permute-done.4
  161.3 3.2 %collective-permute-start.5 = (bf16[256,512]{0,1:T(8,128)(2,1)S(1)}, bf16[256,512]{0,1:T(8,128)(2,1)S(1)}, u32[]{:S(2)}, u32[]{:S(2)}) collective-permute-start(bf16[256,512]{0,1:T(8,128)(2,1)S(1)} %fusion.27), channel_id=1, source_target_pairs={{0,256},{32,288},{64,320},{96,352},{128,384},{160,416},{192,448},{... | collective-permute-start | bytes 786440 | tf_op jit(solution)/shard_map/ppermute | solution.py:12
  164.5 1.0 collective-permute-done.13
  166.0 4.0 %collective-permute-start.14 = (bf16[256,512]{0,1:T(8,128)(2,1)S(1)}, bf16[256,512]{0,1:T(8,128)(2,1)S(1)}, u32[]{:S(2)}, u32[]{:S(2)}) collective-permute-start(bf16[256,512]{0,1:T(8,128)(2,1)S(1)} %fusion.18), channel_id=1, source_target_pairs={{0,128},{32,160},{64,192},{96,224},{128,0},{160,32},{192,64},{224,... | collective-permute-start | bytes 786440 | tf_op jit(solution)/shard_map/ppermute | solution.py:12
  170.0 1.1 collective-permute-done.5
  171.6 4.0 %collective-permute-start.6 = (bf16[256,512]{0,1:T(8,128)(2,1)S(1)}, bf16[256,512]{0,1:T(8,128)(2,1)S(1)}, u32[]{:S(2)}, u32[]{:S(2)}) collective-permute-start(bf16[256,512]{0,1:T(8,128)(2,1)S(1)} %fusion.26), channel_id=1, source_target_pairs={{0,128},{32,160},{64,192},{96,224},{128,0},{160,32},{192,64},{224,... | collective-permute-start | bytes 786440 | tf_op jit(solution)/shard_map/ppermute | solution.py:12
  176.6 3.0 %collective-permute-start.15 = (bf16[256,512]{0,1:T(8,128)(2,1)S(1)}, bf16[256,512]{0,1:T(8,128)(2,1)S(1)}, u32[]{:S(2)}, u32[]{:S(2)}) collective-permute-start(bf16[256,512]{0,1:T(8,128)(2,1)S(1)} %fusion.17), channel_id=1, source_target_pairs={{0,64},{32,96},{64,0},{96,32},{128,192},{160,224},{192,128},{224,1... | collective-permute-start | bytes 786440 | tf_op jit(solution)/shard_map/ppermute | solution.py:12
  179.5 4.7 %collective-permute-done.6 = bf16[256,512]{0,1:T(8,128)(2,1)S(1)} collective-permute-done((bf16[256,512]{0,1:T(8,128)(2,1)S(1)}, bf16[256,512]{0,1:T(8,128)(2,1)S(1)}, u32[]{:S(2)}, u32[]{:S(2)}) %collective-permute-start.6) | collective-permute-done | bytes 262176 | tf_op jit(solution)/shard_map/ppermute | solution.py:12
  184.7 1.9 collective-permute-start.7
  186.7 3.1 %collective-permute-done.15 = bf16[256,512]{0,1:T(8,128)(2,1)S(1)} collective-permute-done((bf16[256,512]{0,1:T(8,128)(2,1)S(1)}, bf16[256,512]{0,1:T(8,128)(2,1)S(1)}, u32[]{:S(2)}, u32[]{:S(2)}) %collective-permute-start.15) | collective-permute-done | bytes 262176 | tf_op jit(solution)/shard_map/ppermute | solution.py:12
  190.3 2.9 %collective-permute-done.7 = bf16[256,512]{0,1:T(8,128)(2,1)S(1)} collective-permute-done((bf16[256,512]{0,1:T(8,128)(2,1)S(1)}, bf16[256,512]{0,1:T(8,128)(2,1)S(1)}, u32[]{:S(2)}, u32[]{:S(2)}) %collective-permute-start.7) | collective-permute-done | bytes 262176 | tf_op jit(solution)/shard_map/ppermute | solution.py:12
  194.1 1.3 copy.5
  (43 shorter events, 10.0 us)
Async XLA Ops:
  0.0 0.9 copy-start
  0.0 10.5 %copy-start.1 = (bf16[8,1,1,256,512]{4,3,2,1,0:T(8,128)(2,1)S(1)}, bf16[8,1,1,256,512]{4,3,2,1,0:T(8,128)(2,1)}, u32[]{:S(2)}) copy-start(bf16[8,1,1,256,512]{4,3,2,1,0:T(8,128)(2,1)} %param.6) | copy-start | bytes 6291460
  3.2 33.4 %collective-permute-start = (bf16[256,512]{1,0:T(8,128)(2,1)S(1)}, bf16[256,512]{1,0:T(8,128)(2,1)S(1)}, u32[]{:S(2)}, u32[]{:S(2)}) collective-permute-start(bf16[256,512]{1,0:T(8,128)(2,1)S(1)} %get-tuple-element.13), channel_id=1, source_target_pairs={{0,16},{1,17},{2,18},{3,19},{4,20},{5,21},{6,22},{7,23},{8,24},{9,... | collective-permute-start | bytes 786440 | tf_op jit(solution)/shard_map/ppermute | solution.py:12
  8.3 12.0 %collective-permute-start.8 = (bf16[256,512]{1,0:T(8,128)(2,1)}, bf16[256,512]{1,0:T(8,128)(2,1)S(1)}, u32[]{:S(2)}, u32[]{:S(2)}) collective-permute-start(bf16[256,512]{1,0:T(8,128)(2,1)} %get-tuple-element.14), channel_id=1, source_target_pairs={{0,16},{1,17},{2,18},{3,19},{4,20},{5,21},{6,22},{7,23},{8,24},{9,... | collective-permute-start | bytes 786440 | tf_op jit(solution)/shard_map/ppermute | solution.py:12
  20.8 29.5 %collective-permute-start.9 = (bf16[256,512]{0,1:T(8,128)(2,1)S(1)}, bf16[256,512]{0,1:T(8,128)(2,1)S(1)}, u32[]{:S(2)}, u32[]{:S(2)}) collective-permute-start(bf16[256,512]{0,1:T(8,128)(2,1)S(1)} %fusion.23), channel_id=1, source_target_pairs={{0,8},{1,9},{2,10},{3,11},{4,12},{5,13},{6,14},{7,15},{8,0},{9,1},... | collective-permute-start | bytes 786440 | tf_op jit(solution)/shard_map/ppermute | solution.py:12
  37.1 36.9 %collective-permute-start.1 = (bf16[256,512]{0,1:T(8,128)(2,1)S(1)}, bf16[256,512]{0,1:T(8,128)(2,1)S(1)}, u32[]{:S(2)}, u32[]{:S(2)}) collective-permute-start(bf16[256,512]{0,1:T(8,128)(2,1)S(1)} %fusion.31), channel_id=1, source_target_pairs={{0,8},{1,9},{2,10},{3,11},{4,12},{5,13},{6,14},{7,15},{8,0},{9,1},... | collective-permute-start | bytes 786440 | tf_op jit(solution)/shard_map/ppermute | solution.py:12
  50.8 70.8 %collective-permute-start.10 = (bf16[256,512]{0,1:T(8,128)(2,1)S(1)}, bf16[256,512]{0,1:T(8,128)(2,1)S(1)}, u32[]{:S(2)}, u32[]{:S(2)}) collective-permute-start(bf16[256,512]{0,1:T(8,128)(2,1)S(1)} %fusion.22), channel_id=1, source_target_pairs={{0,4},{1,5},{2,6},{3,7},{4,0},{5,1},{6,2},{7,3},{8,12},{9,13},{10,... | collective-permute-start | bytes 786440 | tf_op jit(solution)/shard_map/ppermute | solution.py:12
  74.6 52.6 %collective-permute-start.2 = (bf16[256,512]{0,1:T(8,128)(2,1)S(1)}, bf16[256,512]{0,1:T(8,128)(2,1)S(1)}, u32[]{:S(2)}, u32[]{:S(2)}) collective-permute-start(bf16[256,512]{0,1:T(8,128)(2,1)S(1)} %fusion.30), channel_id=1, source_target_pairs={{0,4},{1,5},{2,6},{3,7},{4,0},{5,1},{6,2},{7,3},{8,12},{9,13},{10,... | collective-permute-start | bytes 786440 | tf_op jit(solution)/shard_map/ppermute | solution.py:12
  122.1 21.9 %collective-permute-start.11 = (bf16[256,512]{0,1:T(8,128)(2,1)S(1)}, bf16[256,512]{0,1:T(8,128)(2,1)S(1)}, u32[]{:S(2)}, u32[]{:S(2)}) collective-permute-start(bf16[256,512]{0,1:T(8,128)(2,1)S(1)} %fusion.21), channel_id=1, source_target_pairs={{0,2},{1,3},{2,0},{3,1},{4,6},{5,7},{6,4},{7,5},{8,10},{9,11},{10,... | collective-permute-start | bytes 786440 | tf_op jit(solution)/shard_map/ppermute | solution.py:12
  127.7 21.9 %collective-permute-start.3 = (bf16[256,512]{0,1:T(8,128)(2,1)S(1)}, bf16[256,512]{0,1:T(8,128)(2,1)S(1)}, u32[]{:S(2)}, u32[]{:S(2)}) collective-permute-start(bf16[256,512]{0,1:T(8,128)(2,1)S(1)} %fusion.29), channel_id=1, source_target_pairs={{0,2},{1,3},{2,0},{3,1},{4,6},{5,7},{6,4},{7,5},{8,10},{9,11},{10,... | collective-permute-start | bytes 786440 | tf_op jit(solution)/shard_map/ppermute | solution.py:12
  144.6 11.1 %collective-permute-start.12 = (bf16[256,512]{0,1:T(8,128)(2,1)S(1)}, bf16[256,512]{0,1:T(8,128)(2,1)S(1)}, u32[]{:S(2)}, u32[]{:S(2)}) collective-permute-start(bf16[256,512]{0,1:T(8,128)(2,1)S(1)} %fusion.20), channel_id=1, source_target_pairs={{0,1},{1,0},{2,3},{3,2},{4,5},{5,4},{6,7},{7,6},{8,9},{9,8},{10,11... | collective-permute-start | bytes 786440 | tf_op jit(solution)/shard_map/ppermute | solution.py:12
  150.2 10.6 %collective-permute-start.4 = (bf16[256,512]{0,1:T(8,128)(2,1)S(1)}, bf16[256,512]{0,1:T(8,128)(2,1)S(1)}, u32[]{:S(2)}, u32[]{:S(2)}) collective-permute-start(bf16[256,512]{0,1:T(8,128)(2,1)S(1)} %fusion.28), channel_id=1, source_target_pairs={{0,1},{1,0},{2,3},{3,2},{4,5},{5,4},{6,7},{7,6},{8,9},{9,8},{10,11... | collective-permute-start | bytes 786440 | tf_op jit(solution)/shard_map/ppermute | solution.py:12
  156.2 9.3 %collective-permute-start.13 = (bf16[256,512]{0,1:T(8,128)(2,1)S(1)}, bf16[256,512]{0,1:T(8,128)(2,1)S(1)}, u32[]{:S(2)}, u32[]{:S(2)}) collective-permute-start(bf16[256,512]{0,1:T(8,128)(2,1)S(1)} %fusion.19), channel_id=1, source_target_pairs={{0,256},{32,288},{64,320},{96,352},{128,384},{160,416},{192,448},{... | collective-permute-start | bytes 786440 | tf_op jit(solution)/shard_map/ppermute | solution.py:12
  161.3 9.8 %collective-permute-start.5 = (bf16[256,512]{0,1:T(8,128)(2,1)S(1)}, bf16[256,512]{0,1:T(8,128)(2,1)S(1)}, u32[]{:S(2)}, u32[]{:S(2)}) collective-permute-start(bf16[256,512]{0,1:T(8,128)(2,1)S(1)} %fusion.27), channel_id=1, source_target_pairs={{0,256},{32,288},{64,320},{96,352},{128,384},{160,416},{192,448},{... | collective-permute-start | bytes 786440 | tf_op jit(solution)/shard_map/ppermute | solution.py:12
  166.0 10.0 %collective-permute-start.14 = (bf16[256,512]{0,1:T(8,128)(2,1)S(1)}, bf16[256,512]{0,1:T(8,128)(2,1)S(1)}, u32[]{:S(2)}, u32[]{:S(2)}) collective-permute-start(bf16[256,512]{0,1:T(8,128)(2,1)S(1)} %fusion.18), channel_id=1, source_target_pairs={{0,128},{32,160},{64,192},{96,224},{128,0},{160,32},{192,64},{224,... | collective-permute-start | bytes 786440 | tf_op jit(solution)/shard_map/ppermute | solution.py:12
  171.6 12.6 %collective-permute-start.6 = (bf16[256,512]{0,1:T(8,128)(2,1)S(1)}, bf16[256,512]{0,1:T(8,128)(2,1)S(1)}, u32[]{:S(2)}, u32[]{:S(2)}) collective-permute-start(bf16[256,512]{0,1:T(8,128)(2,1)S(1)} %fusion.26), channel_id=1, source_target_pairs={{0,128},{32,160},{64,192},{96,224},{128,0},{160,32},{192,64},{224,... | collective-permute-start | bytes 786440 | tf_op jit(solution)/shard_map/ppermute | solution.py:12
  176.6 13.3 %collective-permute-start.15 = (bf16[256,512]{0,1:T(8,128)(2,1)S(1)}, bf16[256,512]{0,1:T(8,128)(2,1)S(1)}, u32[]{:S(2)}, u32[]{:S(2)}) collective-permute-start(bf16[256,512]{0,1:T(8,128)(2,1)S(1)} %fusion.17), channel_id=1, source_target_pairs={{0,64},{32,96},{64,0},{96,32},{128,192},{160,224},{192,128},{224,1... | collective-permute-start | bytes 786440 | tf_op jit(solution)/shard_map/ppermute | solution.py:12
  184.7 8.5 %collective-permute-start.7 = (bf16[256,512]{0,1:T(8,128)(2,1)S(1)}, bf16[256,512]{0,1:T(8,128)(2,1)S(1)}, u32[]{:S(2)}, u32[]{:S(2)}) collective-permute-start(bf16[256,512]{0,1:T(8,128)(2,1)S(1)} %fusion.25), channel_id=1, source_target_pairs={{0,64},{32,96},{64,0},{96,32},{128,192},{160,224},{192,128},{224,1... | collective-permute-start | bytes 786440 | tf_op jit(solution)/shard_map/ppermute | solution.py:12
  190.1 3.7 %copy-start.2 = (bf16[1,1,256,256]{3,2,1,0:T(8,128)(2,1)S(1)}, bf16[1,1,256,256]{3,2,1,0:T(8,128)(2,1)}, u32[]{:S(2)}) copy-start(bf16[1,1,256,256]{3,2,1,0:T(8,128)(2,1)} %param.7) | copy-start | bytes 393220
where the time goes:
time: 196 us; the launch traced here: 195 us
  waiting for transfers between devices  96.8 us (49%)
  starting transfers between devices  84.9 us (43%)
  matrix products  10.3 us (5%)
  local copies, waits for them, and re-layouts  3.1 us (2%)
    ppermute x16, waiting for transfers between devices, swapped(): return lax.ppermute(value, axis, pairs)  96.8 us
    ppermute x16, starting transfers between devices, swapped(): return lax.ppermute(value, axis, pairs)  84.9 us
    dot_general x16, matrix products, combine(): jnp.dot(weights[:, :rank_rows], lower_part, preferred_element_type=jnp.fl...  4.28 us
    dot_general x16, matrix products, combine(): jnp.dot(weights[:, rank_rows:], upper_part, preferred_element_type=jnp.fl...  4.12 us
  transfers between devices with their start and end apart: 16, of which 14 were waited for; matrix products, arithmetic and copies ran while one was open for 4% of the time, Pallas kernels for 0%

commit v1 on v0

v1 whole, which is shorter than its diff:
```python
import jax
import jax.numpy as jnp
from jax import lax
from jax.sharding import PartitionSpec as P


LEVELS = 8
RING = 16
HOP = 4
FAR = 1
CHUNKS = 2


def swapped(value, axis, bit):
    mask = 2**bit
    pairs = [(source, source ^ mask) for source in range(lax.axis_size(axis))]
    return lax.ppermute(value, axis, pairs)


def shifted(value, step):
    pairs = [
        (source, source // RING * RING + (source + step) % RING)
        for source in range(lax.axis_size("gy"))
    ]
    return lax.ppermute(value, "gy", pairs)


def partner(state, level_bit, low_bits):
    if level_bit < low_bits:
        return swapped(state, "gx", level_bit)
    return swapped(state, "gy", level_bit - low_bits)


def dot(a, b):
    return jnp.dot(a, b, preferred_element_type=jnp.float32)


def combine(own, other, weights, upper):
    rank_rows = own.shape[0]
    lower_part = jnp.where(upper, other, own)
    upper_part = jnp.where(upper, own, other)
    total = dot(weights[:, :rank_rows], lower_part) + dot(weights[:, rank_rows:], upper_part)
    return total.astype(jnp.bfloat16)


def body(sources, coeff_in, transfer, coeff_out):
    size = lax.axis_size("gx")
    low_bits = size.bit_length() - 1
    nbits = low_bits + lax.axis_size("gy").bit_length() - 1
    position = lax.axis_index("gy") * size + lax.axis_index("gx")

    def upper_at(level):
        return position >> (nbits - 1 - level) & 1 == 1

    def exchange(state, level):
        other = partner(state, nbits - 1 - level, low_bits)
        return combine(state, other, transfer[level, 0, 0], upper_at(level))

    far_weights = partner(transfer[FAR, 0, 0], nbits - 1 - (FAR + 1), low_bits)
    state = dot(coeff_in[0, 0], sources[0, 0].astype(jnp.bfloat16)).astype(jnp.bfloat16)
    width = state.shape[1] // CHUNKS
    chunks = [state[:, k * width : (k + 1) * width] for k in range(CHUNKS)]
    others = []
    for k in range(CHUNKS):
        others.append(partner(chunks[k], nbits - 1, low_bits))
    chunks = [combine(c, o, transfer[0, 0, 0], upper_at(0)) for c, o in zip(chunks, others)]
    half = width // 2
    hops = [(shifted(c, -HOP), shifted(c, HOP)) for c in chunks]
    results = []
    for own, (after, before) in zip(chunks, hops):
        far = jnp.concatenate(
            [shifted(after[:, :half], -HOP), shifted(before[:, half:], HOP)], axis=1
        )
        near_upper = upper_at(FAR + 1)
        near = jnp.where(near_upper, before, after)
        near_far = jnp.where(near_upper, after, before)
        near = combine(near, near_far, far_weights, upper_at(FAR))
        own = combine(own, far, transfer[FAR, 0, 0], upper_at(FAR))
        results.append(combine(own, near, transfer[FAR + 1, 0, 0], near_upper))
    chunks = results
    for level in range(FAR + 2, LEVELS):
        chunks = [exchange(c, level) for c in chunks]
    state = jnp.concatenate(chunks, axis=1)
    return dot(coeff_out[0, 0], state)[None, None]


def solution(mesh):
    placed = (
        P("gy", "gx", None, None),
        P("gy", "gx", None, None),
        P(None, "gy", "gx", None, None),
        P("gy", "gx", None, None),
    )

    return jax.shard_map(
        body, mesh=mesh, in_specs=placed, out_specs=P("gy", "gx", None, None), check_vma=False
    )
```

time: 196 us -> 189 us (0.964)
  the two profiles are of different devices: /device:TPU:2 before, /device:TPU:24 now
where the time goes in v1:
time: 189 us; the launch traced here: 188 us
  starting transfers between devices  88.9 us (47%)
  waiting for transfers between devices  79.6 us (42%)
  matrix products  13.6 us (7%)
  local copies, waits for them, and re-layouts  5.83 us (3%)
    ppermute x13, waiting for transfers between devices, swapped(): return lax.ppermute(value, axis, pairs)  45.3 us
    ppermute x8, starting transfers between devices, shifted(): return lax.ppermute(value, 'gy', pairs)  44.8 us
    ppermute x13, starting transfers between devices, swapped(): return lax.ppermute(value, axis, pairs)  44 us
    ppermute x8, waiting for transfers between devices, shifted(): return lax.ppermute(value, 'gy', pairs)  34.3 us
    dot_general x38, matrix products, dot(): return jnp.dot(a, b, preferred_element_type=jnp.float32)  13.6 us
  transfers between devices with their start and end apart: 21, of which 11 were waited for; matrix products, arithmetic and copies ran while one was open for 8% of the time, Pallas kernels for 0%

profile of v1, /device:TPU:24, one launch (start us, length us, event | category | flops | bytes accessed | tf_op | source)
XLA Modules:
  0.0 188.4 jit_solution(14796726683488088400)
XLA Ops:
  2.5 3.1 %collective-permute-start = (bf16[256,512]{1,0:T(8,128)(2,1)S(1)}, bf16[256,512]{1,0:T(8,128)(2,1)S(1)}, u32[]{:S(2)}, u32[]{:S(2)}) collective-permute-start(bf16[256,512]{1,0:T(8,128)(2,1)S(1)} %get-tuple-element.13), channel_id=1, source_target_pairs={{0,16},{1,17},{2,18},{3,19},{4,20},{5,21},{6,22},{7,23},{8,24},{9,... | collective-permute-start | bytes 786440 | tf_op jit(solution)/shard_map/ppermute | solution.py:17
  5.6 4.2 %collective-permute-start.11 = (bf16[256,512]{1,0:T(8,128)(2,1)S(1)}, bf16[256,512]{1,0:T(8,128)(2,1)S(1)}, u32[]{:S(2)}, u32[]{:S(2)}) collective-permute-start(bf16[256,512]{1,0:T(8,128)(2,1)S(1)} %get-tuple-element.14), channel_id=1, source_target_pairs={{0,16},{1,17},{2,18},{3,19},{4,20},{5,21},{6,22},{7,23},{8,24},{9,... | collective-permute-start | bytes 786440 | tf_op jit(solution)/shard_map/ppermute | solution.py:17
  9.9 1.7 slice_bitcast_fusion
  11.5 3.5 %collective-permute-done = bf16[256,512]{1,0:T(8,128)(2,1)S(1)} collective-permute-done((bf16[256,512]{1,0:T(8,128)(2,1)S(1)}, bf16[256,512]{1,0:T(8,128)(2,1)S(1)}, u32[]{:S(2)}, u32[]{:S(2)}) %collective-permute-start) | collective-permute-done | bytes 262176 | tf_op jit(solution)/shard_map/ppermute | solution.py:17
  15.6 12.7 %collective-permute-start.1 = (bf16[256,512]{0,1:T(8,128)(2,1)S(1)}, bf16[256,512]{0,1:T(8,128)(2,1)}, u32[]{:S(2)}, u32[]{:S(2)}) collective-permute-start(bf16[256,512]{0,1:T(8,128)(2,1)S(1)} %fusion.31), channel_id=1, source_target_pairs={{0,12},{1,13},{2,14},{3,15},{4,0},{5,1},{6,2},{7,3},{8,4},{9,5},{1... | collective-permute-start | bytes 786440 | tf_op jit(solution)/shard_map/ppermute | solution.py:25
  28.4 1.9 %collective-permute-start.2 = (bf16[256,512]{0,1:T(8,128)(2,1)S(1)}, bf16[256,512]{0,1:T(8,128)(2,1)}, u32[]{:S(2)}, u32[]{:S(2)}) collective-permute-start(bf16[256,512]{0,1:T(8,128)(2,1)S(1)} %fusion.31), channel_id=1, source_target_pairs={{0,4},{1,5},{2,6},{3,7},{4,8},{5,9},{6,10},{7,11},{8,12},{9,13},{1... | collective-permute-start | bytes 786440 | tf_op jit(solution)/shard_map/ppermute | solution.py:25
  30.9 7.8 %collective-permute-start.12 = (bf16[256,512]{0,1:T(8,128)(2,1)S(1)}, bf16[256,512]{0,1:T(8,128)(2,1)S(1)}, u32[]{:S(2)}, u32[]{:S(2)}) collective-permute-start(bf16[256,512]{0,1:T(8,128)(2,1)S(1)} %fusion.24), channel_id=1, source_target_pairs={{0,12},{1,13},{2,14},{3,15},{4,0},{5,1},{6,2},{7,3},{8,4},{9,5},{1... | collective-permute-start | bytes 786440 | tf_op jit(solution)/shard_map/ppermute | solution.py:25
  38.7 1.9 %collective-permute-start.13 = (bf16[256,512]{0,1:T(8,128)(2,1)S(1)}, bf16[256,512]{0,1:T(8,128)(2,1)S(1)}, u32[]{:S(2)}, u32[]{:S(2)}) collective-permute-start(bf16[256,512]{0,1:T(8,128)(2,1)S(1)} %fusion.24), channel_id=1, source_target_pairs={{0,4},{1,5},{2,6},{3,7},{4,8},{5,9},{6,10},{7,11},{8,12},{9,13},{1... | collective-permute-start | bytes 786440 | tf_op jit(solution)/shard_map/ppermute | solution.py:25
  40.7 5.5 %collective-permute-start.3 = (bf16[256,512]{1,0:T(8,128)(2,1)S(1)}, bf16[256,512]{1,0:T(8,128)(2,1)S(1)}, u32[]{:S(2)}, u32[]{:S(2)}) collective-permute-start(bf16[256,512]{1,0:T(8,128)(2,1)S(1)} %get-tuple-element.10), channel_id=1, source_target_pairs={{0,4},{1,5},{2,6},{3,7},{4,0},{5,1},{6,2},{7,3},{8,12},{9,13},{10,... | collective-permute-start | bytes 786440 | tf_op jit(solution)/shard_map/ppermute | solution.py:17
  46.2 29.9 %collective-permute-done.1 = bf16[256,512]{0,1:T(8,128)(2,1)} collective-permute-done((bf16[256,512]{0,1:T(8,128)(2,1)S(1)}, bf16[256,512]{0,1:T(8,128)(2,1)}, u32[]{:S(2)}, u32[]{:S(2)}) %collective-permute-start.1) | collective-permute-done | bytes 262176 | tf_op jit(solution)/shard_map/ppermute | solution.py:25
  77.0 8.7 %collective-permute-start.4 = (bf16[256,256]{0,1:T(8,128)(2,1)S(1)}, bf16[256,256]{0,1:T(8,128)(2,1)S(1)}, u32[]{:S(2)}, u32[]{:S(2)}) collective-permute-start(bf16[256,256]{0,1:T(8,128)(2,1)S(1)} %slice.160), channel_id=1, source_target_pairs={{0,12},{1,13},{2,14},{3,15},{4,0},{5,1},{6,2},{7,3},{8,4},{9,5},{1... | collective-permute-start | bytes 393224 | tf_op jit(solution)/shard_map/ppermute | solution.py:25
  86.7 1.9 %collective-permute-start.5 = (bf16[256,256]{0,1:T(8,128)(2,1)S(1)}, bf16[256,256]{0,1:T(8,128)(2,1)S(1)}, u32[]{:S(2)}, u32[]{:S(2)}) collective-permute-start(bf16[256,256]{0,1:T(8,128)(2,1)S(1)} %slice.161), channel_id=1, source_target_pairs={{0,4},{1,5},{2,6},{3,7},{4,8},{5,9},{6,10},{7,11},{8,12},{9,13},{1... | collective-permute-start | bytes 393224 | tf_op jit(solution)/shard_map/ppermute | solution.py:25
  88.6 7.8 %collective-permute-start.14 = (bf16[256,256]{0,1:T(8,128)(2,1)S(1)}, bf16[256,256]{0,1:T(8,128)(2,1)S(1)}, u32[]{:S(2)}, u32[]{:S(2)}) collective-permute-start(bf16[256,256]{0,1:T(8,128)(2,1)S(1)} %slice.177), channel_id=1, source_target_pairs={{0,12},{1,13},{2,14},{3,15},{4,0},{5,1},{6,2},{7,3},{8,4},{9,5},{1... | collective-permute-start | bytes 393224 | tf_op jit(solution)/shard_map/ppermute | solution.py:25
  96.5 1.9 %collective-permute-start.15 = (bf16[256,256]{0,1:T(8,128)(2,1)S(1)}, bf16[256,256]{0,1:T(8,128)(2,1)S(1)}, u32[]{:S(2)}, u32[]{:S(2)}) collective-permute-start(bf16[256,256]{0,1:T(8,128)(2,1)S(1)} %slice.178), channel_id=1, source_target_pairs={{0,4},{1,5},{2,6},{3,7},{4,8},{5,9},{6,10},{7,11},{8,12},{9,13},{1... | collective-permute-start | bytes 393224 | tf_op jit(solution)/shard_map/ppermute | solution.py:25
  98.4 6.2 %collective-permute-done.3 = bf16[256,512]{1,0:T(8,128)(2,1)S(1)} collective-permute-done((bf16[256,512]{1,0:T(8,128)(2,1)S(1)}, bf16[256,512]{1,0:T(8,128)(2,1)S(1)}, u32[]{:S(2)}, u32[]{:S(2)}) %collective-permute-start.3) | collective-permute-done | bytes 262176 | tf_op jit(solution)/shard_map/ppermute | solution.py:17
  107.7 4.3 %collective-permute-done.4 = bf16[256,256]{0,1:T(8,128)(2,1)S(1)} collective-permute-done((bf16[256,256]{0,1:T(8,128)(2,1)S(1)}, bf16[256,256]{0,1:T(8,128)(2,1)S(1)}, u32[]{:S(2)}, u32[]{:S(2)}) %collective-permute-start.4) | collective-permute-done | bytes 131104 | tf_op jit(solution)/shard_map/ppermute | solution.py:25
  113.2 1.9 %collective-permute-start.6 = (bf16[256,512]{0,1:T(8,128)(2,1)S(1)}, bf16[256,512]{0,1:T(8,128)(2,1)S(1)}, u32[]{:S(2)}, u32[]{:S(2)}) collective-permute-start(bf16[256,512]{0,1:T(8,128)(2,1)S(1)} %fusion.30), channel_id=1, source_target_pairs={{0,2},{1,3},{2,0},{3,1},{4,6},{5,7},{6,4},{7,5},{8,10},{9,11},{10,... | collective-permute-start | bytes 786440 | tf_op jit(solution)/shard_map/ppermute | solution.py:17
  116.2 4.8 %collective-permute-start.16 = (bf16[256,512]{0,1:T(8,128)(2,1)S(1)}, bf16[256,512]{0,1:T(8,128)(2,1)S(1)}, u32[]{:S(2)}, u32[]{:S(2)}) collective-permute-start(bf16[256,512]{0,1:T(8,128)(2,1)S(1)} %fusion.23), channel_id=1, source_target_pairs={{0,2},{1,3},{2,0},{3,1},{4,6},{5,7},{6,4},{7,5},{8,10},{9,11},{10,... | collective-permute-start | bytes 786440 | tf_op jit(solution)/shard_map/ppermute | solution.py:17
  121.1 14.6 %collective-permute-done.6 = bf16[256,512]{0,1:T(8,128)(2,1)S(1)} collective-permute-done((bf16[256,512]{0,1:T(8,128)(2,1)S(1)}, bf16[256,512]{0,1:T(8,128)(2,1)S(1)}, u32[]{:S(2)}, u32[]{:S(2)}) %collective-permute-start.6) | collective-permute-done | bytes 262176 | tf_op jit(solution)/shard_map/ppermute | solution.py:17
  136.2 1.9 %collective-permute-start.7 = (bf16[256,512]{0,1:T(8,128)(2,1)S(1)}, bf16[256,512]{0,1:T(8,128)(2,1)S(1)}, u32[]{:S(2)}, u32[]{:S(2)}) collective-permute-start(bf16[256,512]{0,1:T(8,128)(2,1)S(1)} %fusion.29), channel_id=1, source_target_pairs={{0,1},{1,0},{2,3},{3,2},{4,5},{5,4},{6,7},{7,6},{8,9},{9,8},{10,11... | collective-permute-start | bytes 786440 | tf_op jit(solution)/shard_map/ppermute | solution.py:17
  139.8 2.8 %collective-permute-start.17 = (bf16[256,512]{0,1:T(8,128)(2,1)S(1)}, bf16[256,512]{0,1:T(8,128)(2,1)S(1)}, u32[]{:S(2)}, u32[]{:S(2)}) collective-permute-start(bf16[256,512]{0,1:T(8,128)(2,1)S(1)} %fusion.22), channel_id=1, source_target_pairs={{0,1},{1,0},{2,3},{3,2},{4,5},{5,4},{6,7},{7,6},{8,9},{9,8},{10,11... | collective-permute-start | bytes 786440 | tf_op jit(solution)/shard_map/ppermute | solution.py:17
  142.6 4.7 %collective-permute-done.7 = bf16[256,512]{0,1:T(8,128)(2,1)S(1)} collective-permute-done((bf16[256,512]{0,1:T(8,128)(2,1)S(1)}, bf16[256,512]{0,1:T(8,128)(2,1)S(1)}, u32[]{:S(2)}, u32[]{:S(2)}) %collective-permute-start.7) | collective-permute-done | bytes 262176 | tf_op jit(solution)/shard_map/ppermute | solution.py:17
  147.8 2.7 %collective-permute-start.8 = (bf16[256,512]{0,1:T(8,128)(2,1)S(1)}, bf16[256,512]{0,1:T(8,128)(2,1)S(1)}, u32[]{:S(2)}, u32[]{:S(2)}) collective-permute-start(bf16[256,512]{0,1:T(8,128)(2,1)S(1)} %fusion.28), channel_id=1, source_target_pairs={{0,256},{32,288},{64,320},{96,352},{128,384},{160,416},{192,448},{... | collective-permute-start | bytes 786440 | tf_op jit(solution)/shard_map/ppermute | solution.py:17
  151.1 3.2 %collective-permute-start.18 = (bf16[256,512]{0,1:T(8,128)(2,1)S(1)}, bf16[256,512]{0,1:T(8,128)(2,1)S(1)}, u32[]{:S(2)}, u32[]{:S(2)}) collective-permute-start(bf16[256,512]{0,1:T(8,128)(2,1)S(1)} %fusion.21), channel_id=1, source_target_pairs={{0,256},{32,288},{64,320},{96,352},{128,384},{160,416},{192,448},{... | collective-permute-start | bytes 786440 | tf_op jit(solution)/shard_map/ppermute | solution.py:17
  154.3 4.4 %collective-permute-done.8 = bf16[256,512]{0,1:T(8,128)(2,1)S(1)} collective-permute-done((bf16[256,512]{0,1:T(8,128)(2,1)S(1)}, bf16[256,512]{0,1:T(8,128)(2,1)S(1)}, u32[]{:S(2)}, u32[]{:S(2)}) %collective-permute-start.8) | collective-permute-done | bytes 262176 | tf_op jit(solution)/shard_map/ppermute | solution.py:17
  159.2 4.8 %collective-permute-start.9 = (bf16[256,512]{0,1:T(8,128)(2,1)S(1)}, bf16[256,512]{0,1:T(8,128)(2,1)S(1)}, u32[]{:S(2)}, u32[]{:S(2)}) collective-permute-start(bf16[256,512]{0,1:T(8,128)(2,1)S(1)} %fusion.27), channel_id=1, source_target_pairs={{0,128},{32,160},{64,192},{96,224},{128,0},{160,32},{192,64},{224,... | collective-permute-start | bytes 786440 | tf_op jit(solution)/shard_map/ppermute | solution.py:17
  164.6 2.6 %collective-permute-start.19 = (bf16[256,512]{0,1:T(8,128)(2,1)S(1)}, bf16[256,512]{0,1:T(8,128)(2,1)S(1)}, u32[]{:S(2)}, u32[]{:S(2)}) collective-permute-start(bf16[256,512]{0,1:T(8,128)(2,1)S(1)} %fusion.20), channel_id=1, source_target_pairs={{0,128},{32,160},{64,192},{96,224},{128,0},{160,32},{192,64},{224,... | collective-permute-start | bytes 786440 | tf_op jit(solution)/shard_map/ppermute | solution.py:17
  167.1 4.7 %collective-permute-done.9 = bf16[256,512]{0,1:T(8,128)(2,1)S(1)} collective-permute-done((bf16[256,512]{0,1:T(8,128)(2,1)S(1)}, bf16[256,512]{0,1:T(8,128)(2,1)S(1)}, u32[]{:S(2)}, u32[]{:S(2)}) %collective-permute-start.9) | collective-permute-done | bytes 262176 | tf_op jit(solution)/shard_map/ppermute | solution.py:17
  172.4 3.3 %collective-permute-start.10 = (bf16[256,512]{0,1:T(8,128)(2,1)S(1)}, bf16[256,512]{0,1:T(8,128)(2,1)S(1)}, u32[]{:S(2)}, u32[]{:S(2)}) collective-permute-start(bf16[256,512]{0,1:T(8,128)(2,1)S(1)} %fusion.26), channel_id=1, source_target_pairs={{0,64},{32,96},{64,0},{96,32},{128,192},{160,224},{192,128},{224,1... | collective-permute-start | bytes 786440 | tf_op jit(solution)/shard_map/ppermute | solution.py:17
  175.6 1.8 collective-permute-done.19
  178.0 3.3 %collective-permute-start.20 = (bf16[256,512]{0,1:T(8,128)(2,1)S(1)}, bf16[256,512]{0,1:T(8,128)(2,1)S(1)}, u32[]{:S(2)}, u32[]{:S(2)}) collective-permute-start(bf16[256,512]{0,1:T(8,128)(2,1)S(1)} %fusion.19), channel_id=1, source_target_pairs={{0,64},{32,96},{64,0},{96,32},{128,192},{160,224},{192,128},{224,1... | collective-permute-start | bytes 786440 | tf_op jit(solution)/shard_map/ppermute | solution.py:17
  181.8 4.4 %collective-permute-done.20 = bf16[256,512]{0,1:T(8,128)(2,1)S(1)} collective-permute-done((bf16[256,512]{0,1:T(8,128)(2,1)S(1)}, bf16[256,512]{0,1:T(8,128)(2,1)S(1)}, u32[]{:S(2)}, u32[]{:S(2)}) %collective-permute-start.20) | collective-permute-done | bytes 262176 | tf_op jit(solution)/shard_map/ppermute | solution.py:17
  (63 shorter events, 18.9 us)
Async XLA Ops:
  0.0 0.9 copy-start
  2.5 12.6 %collective-permute-start = (bf16[256,512]{1,0:T(8,128)(2,1)S(1)}, bf16[256,512]{1,0:T(8,128)(2,1)S(1)}, u32[]{:S(2)}, u32[]{:S(2)}) collective-permute-start(bf16[256,512]{1,0:T(8,128)(2,1)S(1)} %get-tuple-element.13), channel_id=1, source_target_pairs={{0,16},{1,17},{2,18},{3,19},{4,20},{5,21},{6,22},{7,23},{8,24},{9,... | collective-permute-start | bytes 786440 | tf_op jit(solution)/shard_map/ppermute | solution.py:17
  5.6 24.7 %collective-permute-start.11 = (bf16[256,512]{1,0:T(8,128)(2,1)S(1)}, bf16[256,512]{1,0:T(8,128)(2,1)S(1)}, u32[]{:S(2)}, u32[]{:S(2)}) collective-permute-start(bf16[256,512]{1,0:T(8,128)(2,1)S(1)} %get-tuple-element.14), channel_id=1, source_target_pairs={{0,16},{1,17},{2,18},{3,19},{4,20},{5,21},{6,22},{7,23},{8,24},{9,... | collective-permute-start | bytes 786440 | tf_op jit(solution)/shard_map/ppermute | solution.py:17
  15.6 60.4 %collective-permute-start.1 = (bf16[256,512]{0,1:T(8,128)(2,1)S(1)}, bf16[256,512]{0,1:T(8,128)(2,1)}, u32[]{:S(2)}, u32[]{:S(2)}) collective-permute-start(bf16[256,512]{0,1:T(8,128)(2,1)S(1)} %fusion.31), channel_id=1, source_target_pairs={{0,12},{1,13},{2,14},{3,15},{4,0},{5,1},{6,2},{7,3},{8,4},{9,5},{1... | collective-permute-start | bytes 786440 | tf_op jit(solution)/shard_map/ppermute | solution.py:25
  28.4 57.4 %collective-permute-start.2 = (bf16[256,512]{0,1:T(8,128)(2,1)S(1)}, bf16[256,512]{0,1:T(8,128)(2,1)}, u32[]{:S(2)}, u32[]{:S(2)}) collective-permute-start(bf16[256,512]{0,1:T(8,128)(2,1)S(1)} %fusion.31), channel_id=1, source_target_pairs={{0,4},{1,5},{2,6},{3,7},{4,8},{5,9},{6,10},{7,11},{8,12},{9,13},{1... | collective-permute-start | bytes 786440 | tf_op jit(solution)/shard_map/ppermute | solution.py:25
  30.9 57.7 %collective-permute-start.12 = (bf16[256,512]{0,1:T(8,128)(2,1)S(1)}, bf16[256,512]{0,1:T(8,128)(2,1)S(1)}, u32[]{:S(2)}, u32[]{:S(2)}) collective-permute-start(bf16[256,512]{0,1:T(8,128)(2,1)S(1)} %fusion.24), channel_id=1, source_target_pairs={{0,12},{1,13},{2,14},{3,15},{4,0},{5,1},{6,2},{7,3},{8,4},{9,5},{1... | collective-permute-start | bytes 786440 | tf_op jit(solution)/shard_map/ppermute | solution.py:25
  38.7 57.7 %collective-permute-start.13 = (bf16[256,512]{0,1:T(8,128)(2,1)S(1)}, bf16[256,512]{0,1:T(8,128)(2,1)S(1)}, u32[]{:S(2)}, u32[]{:S(2)}) collective-permute-start(bf16[256,512]{0,1:T(8,128)(2,1)S(1)} %fusion.24), channel_id=1, source_target_pairs={{0,4},{1,5},{2,6},{3,7},{4,8},{5,9},{6,10},{7,11},{8,12},{9,13},{1... | collective-permute-start | bytes 786440 | tf_op jit(solution)/shard_map/ppermute | solution.py:25
  40.7 63.9 %collective-permute-start.3 = (bf16[256,512]{1,0:T(8,128)(2,1)S(1)}, bf16[256,512]{1,0:T(8,128)(2,1)S(1)}, u32[]{:S(2)}, u32[]{:S(2)}) collective-permute-start(bf16[256,512]{1,0:T(8,128)(2,1)S(1)} %get-tuple-element.10), channel_id=1, source_target_pairs={{0,4},{1,5},{2,6},{3,7},{4,0},{5,1},{6,2},{7,3},{8,12},{9,13},{10,... | collective-permute-start | bytes 786440 | tf_op jit(solution)/shard_map/ppermute | solution.py:17
  77.0 35.0 %collective-permute-start.4 = (bf16[256,256]{0,1:T(8,128)(2,1)S(1)}, bf16[256,256]{0,1:T(8,128)(2,1)S(1)}, u32[]{:S(2)}, u32[]{:S(2)}) collective-permute-start(bf16[256,256]{0,1:T(8,128)(2,1)S(1)} %slice.160), channel_id=1, source_target_pairs={{0,12},{1,13},{2,14},{3,15},{4,0},{5,1},{6,2},{7,3},{8,4},{9,5},{1... | collective-permute-start | bytes 393224 | tf_op jit(solution)/shard_map/ppermute | solution.py:25
  86.7 25.4 %collective-permute-start.5 = (bf16[256,256]{0,1:T(8,128)(2,1)S(1)}, bf16[256,256]{0,1:T(8,128)(2,1)S(1)}, u32[]{:S(2)}, u32[]{:S(2)}) collective-permute-start(bf16[256,256]{0,1:T(8,128)(2,1)S(1)} %slice.161), channel_id=1, source_target_pairs={{0,4},{1,5},{2,6},{3,7},{4,8},{5,9},{6,10},{7,11},{8,12},{9,13},{1... | collective-permute-start | bytes 393224 | tf_op jit(solution)/shard_map/ppermute | solution.py:25
  88.6 26.5 %collective-permute-start.14 = (bf16[256,256]{0,1:T(8,128)(2,1)S(1)}, bf16[256,256]{0,1:T(8,128)(2,1)S(1)}, u32[]{:S(2)}, u32[]{:S(2)}) collective-permute-start(bf16[256,256]{0,1:T(8,128)(2,1)S(1)} %slice.177), channel_id=1, source_target_pairs={{0,12},{1,13},{2,14},{3,15},{4,0},{5,1},{6,2},{7,3},{8,4},{9,5},{1... | collective-permute-start | bytes 393224 | tf_op jit(solution)/shard_map/ppermute | solution.py:25
  96.5 18.6 %collective-permute-start.15 = (bf16[256,256]{0,1:T(8,128)(2,1)S(1)}, bf16[256,256]{0,1:T(8,128)(2,1)S(1)}, u32[]{:S(2)}, u32[]{:S(2)}) collective-permute-start(bf16[256,256]{0,1:T(8,128)(2,1)S(1)} %slice.178), channel_id=1, source_target_pairs={{0,4},{1,5},{2,6},{3,7},{4,8},{5,9},{6,10},{7,11},{8,12},{9,13},{1... | collective-permute-start | bytes 393224 | tf_op jit(solution)/shard_map/ppermute | solution.py:25
  113.2 22.5 %collective-permute-start.6 = (bf16[256,512]{0,1:T(8,128)(2,1)S(1)}, bf16[256,512]{0,1:T(8,128)(2,1)S(1)}, u32[]{:S(2)}, u32[]{:S(2)}) collective-permute-start(bf16[256,512]{0,1:T(8,128)(2,1)S(1)} %fusion.30), channel_id=1, source_target_pairs={{0,2},{1,3},{2,0},{3,1},{4,6},{5,7},{6,4},{7,5},{8,10},{9,11},{10,... | collective-permute-start | bytes 786440 | tf_op jit(solution)/shard_map/ppermute | solution.py:17
  116.2 23.0 %collective-permute-start.16 = (bf16[256,512]{0,1:T(8,128)(2,1)S(1)}, bf16[256,512]{0,1:T(8,128)(2,1)S(1)}, u32[]{:S(2)}, u32[]{:S(2)}) collective-permute-start(bf16[256,512]{0,1:T(8,128)(2,1)S(1)} %fusion.23), channel_id=1, source_target_pairs={{0,2},{1,3},{2,0},{3,1},{4,6},{5,7},{6,4},{7,5},{8,10},{9,11},{10,... | collective-permute-start | bytes 786440 | tf_op jit(solution)/shard_map/ppermute | solution.py:17
  136.2 11.1 %collective-permute-start.7 = (bf16[256,512]{0,1:T(8,128)(2,1)S(1)}, bf16[256,512]{0,1:T(8,128)(2,1)S(1)}, u32[]{:S(2)}, u32[]{:S(2)}) collective-permute-start(bf16[256,512]{0,1:T(8,128)(2,1)S(1)} %fusion.29), channel_id=1, source_target_pairs={{0,1},{1,0},{2,3},{3,2},{4,5},{5,4},{6,7},{7,6},{8,9},{9,8},{10,11... | collective-permute-start | bytes 786440 | tf_op jit(solution)/shard_map/ppermute | solution.py:17
  139.8 10.7 %collective-permute-start.17 = (bf16[256,512]{0,1:T(8,128)(2,1)S(1)}, bf16[256,512]{0,1:T(8,128)(2,1)S(1)}, u32[]{:S(2)}, u32[]{:S(2)}) collective-permute-start(bf16[256,512]{0,1:T(8,128)(2,1)S(1)} %fusion.22), channel_id=1, source_target_pairs={{0,1},{1,0},{2,3},{3,2},{4,5},{5,4},{6,7},{7,6},{8,9},{9,8},{10,11... | collective-permute-start | bytes 786440 | tf_op jit(solution)/shard_map/ppermute | solution.py:17
  147.8 10.8 %collective-permute-start.8 = (bf16[256,512]{0,1:T(8,128)(2,1)S(1)}, bf16[256,512]{0,1:T(8,128)(2,1)S(1)}, u32[]{:S(2)}, u32[]{:S(2)}) collective-permute-start(bf16[256,512]{0,1:T(8,128)(2,1)S(1)} %fusion.28), channel_id=1, source_target_pairs={{0,256},{32,288},{64,320},{96,352},{128,384},{160,416},{192,448},{... | collective-permute-start | bytes 786440 | tf_op jit(solution)/shard_map/ppermute | solution.py:17
  151.1 13.0 %collective-permute-start.18 = (bf16[256,512]{0,1:T(8,128)(2,1)S(1)}, bf16[256,512]{0,1:T(8,128)(2,1)S(1)}, u32[]{:S(2)}, u32[]{:S(2)}) collective-permute-start(bf16[256,512]{0,1:T(8,128)(2,1)S(1)} %fusion.21), channel_id=1, source_target_pairs={{0,256},{32,288},{64,320},{96,352},{128,384},{160,416},{192,448},{... | collective-permute-start | bytes 786440 | tf_op jit(solution)/shard_map/ppermute | solution.py:17
  159.2 12.6 %collective-permute-start.9 = (bf16[256,512]{0,1:T(8,128)(2,1)S(1)}, bf16[256,512]{0,1:T(8,128)(2,1)S(1)}, u32[]{:S(2)}, u32[]{:S(2)}) collective-permute-start(bf16[256,512]{0,1:T(8,128)(2,1)S(1)} %fusion.27), channel_id=1, source_target_pairs={{0,128},{32,160},{64,192},{96,224},{128,0},{160,32},{192,64},{224,... | collective-permute-start | bytes 786440 | tf_op jit(solution)/shard_map/ppermute | solution.py:17
  164.6 12.8 %collective-permute-start.19 = (bf16[256,512]{0,1:T(8,128)(2,1)S(1)}, bf16[256,512]{0,1:T(8,128)(2,1)S(1)}, u32[]{:S(2)}, u32[]{:S(2)}) collective-permute-start(bf16[256,512]{0,1:T(8,128)(2,1)S(1)} %fusion.20), channel_id=1, source_target_pairs={{0,128},{32,160},{64,192},{96,224},{128,0},{160,32},{192,64},{224,... | collective-permute-start | bytes 786440 | tf_op jit(solution)/shard_map/ppermute | solution.py:17
  172.4 8.9 %collective-permute-start.10 = (bf16[256,512]{0,1:T(8,128)(2,1)S(1)}, bf16[256,512]{0,1:T(8,128)(2,1)S(1)}, u32[]{:S(2)}, u32[]{:S(2)}) collective-permute-start(bf16[256,512]{0,1:T(8,128)(2,1)S(1)} %fusion.26), channel_id=1, source_target_pairs={{0,64},{32,96},{64,0},{96,32},{128,192},{160,224},{192,128},{224,1... | collective-permute-start | bytes 786440 | tf_op jit(solution)/shard_map/ppermute | solution.py:17
  178.0 8.3 %collective-permute-start.20 = (bf16[256,512]{0,1:T(8,128)(2,1)S(1)}, bf16[256,512]{0,1:T(8,128)(2,1)S(1)}, u32[]{:S(2)}, u32[]{:S(2)}) collective-permute-start(bf16[256,512]{0,1:T(8,128)(2,1)S(1)} %fusion.19), channel_id=1, source_target_pairs={{0,64},{32,96},{64,0},{96,32},{128,192},{160,224},{192,128},{224,1... | collective-permute-start | bytes 786440 | tf_op jit(solution)/shard_map/ppermute | solution.py:17
  181.5 5.2 %copy-start.1 = (bf16[1,1,256,256]{3,2,1,0:T(8,128)(2,1)S(1)}, bf16[1,1,256,256]{3,2,1,0:T(8,128)(2,1)}, u32[]{:S(2)}) copy-start(bf16[1,1,256,256]{3,2,1,0:T(8,128)(2,1)} %param.7) | copy-start | bytes 393220

commit v2 on v1

--- a/solution.py
+++ b/solution.py
@@ -1,6 +1,8 @@
 import jax
 import jax.numpy as jnp
 from jax import lax
+from jax.experimental import pallas as pl
+from jax.experimental.pallas import tpu as pltpu
 from jax.sharding import PartitionSpec as P
 
 
@@ -9,6 +11,8 @@
 HOP = 4
 FAR = 1
 CHUNKS = 2
+BLOCK = 256
+FINISH_BYTES = 8 * 1024 * 1024
 
 
 def swapped(value, axis, bit):
@@ -43,6 +47,61 @@
     return total.astype(jnp.bfloat16)
 
 
+def finish_kernel(flag_ref, w_ref, c_ref, own_ref, other_ref, *refs):
+    out_ref, state_ref = refs[-2:]
+    rank = own_ref.shape[0]
+    width = out_ref.shape[1]
+    left, right = w_ref[:, :rank], w_ref[:, rank:]
+    here = pl.ds(pl.multiple_of(pl.program_id(0) * width, width), width)
+    own, other = own_ref[:, here], other_ref[:, here]
+
+    @pl.when(flag_ref[0] == 0)
+    def _():
+        total = dot(left, own) + dot(right, other)
+        state_ref[...] = total.astype(jnp.bfloat16)
+
+    @pl.when(flag_ref[0] != 0)
+    def _():
+        total = dot(left, other) + dot(right, own)
+        state_ref[...] = total.astype(jnp.bfloat16)
+
+    out_ref[...] = dot(c_ref[...], state_ref[...])
+
+
+def finish(flag, weights, coeff, own, other, held, begin, cols):
+    rank, width = own.shape
+    rows = coeff.shape[0]
+    block = min(width, BLOCK)
+    inputs = [flag, weights, coeff, own, other]
+    specs = [
+        pl.BlockSpec(memory_space=pltpu.SMEM),
+        pl.BlockSpec(memory_space=pltpu.VMEM),
+        pl.BlockSpec(memory_space=pltpu.VMEM),
+        pl.BlockSpec(memory_space=pltpu.VMEM),
+        pl.BlockSpec(memory_space=pltpu.VMEM),
+    ]
+    aliases = {}
+    if held is not None:
+        inputs.append(held)
+        specs.append(pl.BlockSpec(memory_space=pl.ANY))
+        aliases = {5: 0}
+    return pl.pallas_call(
+        finish_kernel,
+        grid=(width // block,),
+        in_specs=specs,
+        out_specs=pl.BlockSpec((rows, block), lambda i: (0, begin // block + i)),
+        out_shape=jax.ShapeDtypeStruct((rows, cols), jnp.float32),
+        scratch_shapes=[pltpu.VMEM((rank, block), jnp.bfloat16)],
+        input_output_aliases=aliases,
+        compiler_params=pltpu.CompilerParams(vmem_limit_bytes=FINISH_BYTES),
+        cost_estimate=pl.CostEstimate(
+            flops=2 * rank * width * (2 * rank + rows),
+            bytes_accessed=4 * rows * width,
+            transcendentals=0,
+        ),
+    )(*inputs)
+
+
 def body(sources, coeff_in, transfer, coeff_out):
     size = lax.axis_size("gx")
     low_bits = size.bit_length() - 1
@@ -51,10 +110,6 @@
 
     def upper_at(level):
         return position >> (nbits - 1 - level) & 1 == 1
-
-    def exchange(state, level):
-        other = partner(state, nbits - 1 - level, low_bits)
-        return combine(state, other, transfer[level, 0, 0], upper_at(level))
 
     far_weights = partner(transfer[FAR, 0, 0], nbits - 1 - (FAR + 1), low_bits)
     state = dot(coeff_in[0, 0], sources[0, 0].astype(jnp.bfloat16)).astype(jnp.bfloat16)
@@ -65,23 +120,40 @@
         others.append(partner(chunks[k], nbits - 1, low_bits))
     chunks = [combine(c, o, transfer[0, 0, 0], upper_at(0)) for c, o in zip(chunks, others)]
     half = width // 2
-    hops = [(shifted(c, -HOP), shifted(c, HOP)) for c in chunks]
+    hops = []
+    for chunk in chunks:
+        after = shifted(chunk, -HOP)
+        before = shifted(chunk, HOP)
+        hops.append((after, before))
+    near_upper = upper_at(FAR + 1)
     results = []
     for own, (after, before) in zip(chunks, hops):
-        far = jnp.concatenate(
-            [shifted(after[:, :half], -HOP), shifted(before[:, half:], HOP)], axis=1
-        )
-        near_upper = upper_at(FAR + 1)
+        ahead = shifted(after[:, :half], -HOP)
+        behind = shifted(before[:, half:], HOP)
+        far = jnp.concatenate([ahead, behind], axis=1)
+        own = combine(own, far, transfer[FAR, 0, 0], upper_at(FAR))
         near = jnp.where(near_upper, before, after)
         near_far = jnp.where(near_upper, after, before)
         near = combine(near, near_far, far_weights, upper_at(FAR))
-        own = combine(own, far, transfer[FAR, 0, 0], upper_at(FAR))
         results.append(combine(own, near, transfer[FAR + 1, 0, 0], near_upper))
     chunks = results
-    for level in range(FAR + 2, LEVELS):
-        chunks = [exchange(c, level) for c in chunks]
-    state = jnp.concatenate(chunks, axis=1)
-    return dot(coeff_out[0, 0], state)[None, None]
+    for level in range(FAR + 2, LEVELS - 1):
+        others = []
+        for k in range(CHUNKS):
+            others.append(partner(chunks[k], nbits - 1 - level, low_bits))
+        chunks = [
+            combine(c, o, transfer[level, 0, 0], upper_at(level)) for c, o in zip(chunks, others)
+        ]
+    level = LEVELS - 1
+    flag = upper_at(level).astype(jnp.int32).reshape(1)
+    others = [partner(c, nbits - 1 - level, low_bits) for c in chunks]
+    result = None
+    for k in range(CHUNKS):
+        result = finish(
+            flag, transfer[level, 0, 0], coeff_out[0, 0], chunks[k], others[k],
+            result, k * width, CHUNKS * width,
+        )
+    return result[None, None]
 
 
 def solution(mesh):

time: 189 us -> 191 us (1.011)
  the two profiles are of different devices: /device:TPU:24 before, /device:TPU:12 now
where the time goes in v2:
time: 191 us; the launch traced here: 190 us
  starting transfers between devices  87.7 us (46%)
  waiting for transfers between devices  81.9 us (43%)
  matrix products  12.1 us (6%)
  local copies, waits for them, and re-layouts  4.51 us (2%)
  Pallas kernels  3.23 us (2%)
    ppermute x13, waiting for transfers between devices, swapped(): return lax.ppermute(value, axis, pairs)  51.5 us
    ppermute x8, starting transfers between devices, shifted(): return lax.ppermute(value, 'gy', pairs)  44.9 us
    ppermute x13, starting transfers between devices, swapped(): return lax.ppermute(value, axis, pairs)  42.8 us
    ppermute x8, waiting for transfers between devices, shifted(): return lax.ppermute(value, 'gy', pairs)  30.4 us
    dot_general x33, matrix products, dot(): return jnp.dot(a, b, preferred_element_type=jnp.float32)  12.1 us
  transfers between devices with their start and end apart: 21, of which 13 were waited for; matrix products, arithmetic and copies ran while one was open for 7% of the time, Pallas kernels for 1%

profile of v2, /device:TPU:12, one launch (start us, length us, event | category | flops | bytes accessed | tf_op | source)
XLA Modules:
  0.0 189.9 jit_solution(2664168675903794229)
XLA Ops:
  2.5 4.2 %collective-permute-start = (bf16[256,512]{1,0:T(8,128)(2,1)S(1)}, bf16[256,512]{1,0:T(8,128)(2,1)S(1)}, u32[]{:S(2)}, u32[]{:S(2)}) collective-permute-start(bf16[256,512]{1,0:T(8,128)(2,1)S(1)} %get-tuple-element.14), channel_id=1, source_target_pairs={{0,16},{1,17},{2,18},{3,19},{4,20},{5,21},{6,22},{7,23},{8,24},{9,... | collective-permute-start | bytes 786440 | tf_op jit(solution)/shard_map/ppermute | solution.py:21
  6.7 3.1 %collective-permute-start.11 = (bf16[256,512]{1,0:T(8,128)(2,1)S(1)}, bf16[256,512]{1,0:T(8,128)(2,1)S(1)}, u32[]{:S(2)}, u32[]{:S(2)}) collective-permute-start(bf16[256,512]{1,0:T(8,128)(2,1)S(1)} %get-tuple-element.13), channel_id=1, source_target_pairs={{0,16},{1,17},{2,18},{3,19},{4,20},{5,21},{6,22},{7,23},{8,24},{9,... | collective-permute-start | bytes 786440 | tf_op jit(solution)/shard_map/ppermute | solution.py:21
  9.9 1.7 slice_bitcast_fusion
  11.5 3.5 %collective-permute-done = bf16[256,512]{1,0:T(8,128)(2,1)S(1)} collective-permute-done((bf16[256,512]{1,0:T(8,128)(2,1)S(1)}, bf16[256,512]{1,0:T(8,128)(2,1)S(1)}, u32[]{:S(2)}, u32[]{:S(2)}) %collective-permute-start) | collective-permute-done | bytes 262176 | tf_op jit(solution)/shard_map/ppermute | solution.py:21
  15.6 12.7 %collective-permute-start.1 = (bf16[256,512]{0,1:T(8,128)(2,1)S(1)}, bf16[256,512]{0,1:T(8,128)(2,1)}, u32[]{:S(2)}, u32[]{:S(2)}) collective-permute-start(bf16[256,512]{0,1:T(8,128)(2,1)S(1)} %fusion.27), channel_id=1, source_target_pairs={{0,12},{1,13},{2,14},{3,15},{4,0},{5,1},{6,2},{7,3},{8,4},{9,5},{1... | collective-permute-start | bytes 786440 | tf_op jit(solution)/shard_map/ppermute | solution.py:29
  28.4 1.9 %collective-permute-start.2 = (bf16[256,512]{0,1:T(8,128)(2,1)S(1)}, bf16[256,512]{0,1:T(8,128)(2,1)}, u32[]{:S(2)}, u32[]{:S(2)}) collective-permute-start(bf16[256,512]{0,1:T(8,128)(2,1)S(1)} %fusion.27), channel_id=1, source_target_pairs={{0,4},{1,5},{2,6},{3,7},{4,8},{5,9},{6,10},{7,11},{8,12},{9,13},{1... | collective-permute-start | bytes 786440 | tf_op jit(solution)/shard_map/ppermute | solution.py:29
  30.9 7.8 %collective-permute-start.12 = (bf16[256,512]{0,1:T(8,128)(2,1)S(1)}, bf16[256,512]{0,1:T(8,128)(2,1)S(1)}, u32[]{:S(2)}, u32[]{:S(2)}) collective-permute-start(bf16[256,512]{0,1:T(8,128)(2,1)S(1)} %fusion.21), channel_id=1, source_target_pairs={{0,12},{1,13},{2,14},{3,15},{4,0},{5,1},{6,2},{7,3},{8,4},{9,5},{1... | collective-permute-start | bytes 786440 | tf_op jit(solution)/shard_map/ppermute | solution.py:29
  38.7 1.9 %collective-permute-start.13 = (bf16[256,512]{0,1:T(8,128)(2,1)S(1)}, bf16[256,512]{0,1:T(8,128)(2,1)S(1)}, u32[]{:S(2)}, u32[]{:S(2)}) collective-permute-start(bf16[256,512]{0,1:T(8,128)(2,1)S(1)} %fusion.21), channel_id=1, source_target_pairs={{0,4},{1,5},{2,6},{3,7},{4,8},{5,9},{6,10},{7,11},{8,12},{9,13},{1... | collective-permute-start | bytes 786440 | tf_op jit(solution)/shard_map/ppermute | solution.py:29
  40.7 5.5 %collective-permute-start.3 = (bf16[256,512]{1,0:T(8,128)(2,1)S(1)}, bf16[256,512]{1,0:T(8,128)(2,1)S(1)}, u32[]{:S(2)}, u32[]{:S(2)}) collective-permute-start(bf16[256,512]{1,0:T(8,128)(2,1)S(1)} %get-tuple-element.9), channel_id=1, source_target_pairs={{0,4},{1,5},{2,6},{3,7},{4,0},{5,1},{6,2},{7,3},{8,12},{9,13},{10,... | collective-permute-start | bytes 786440 | tf_op jit(solution)/shard_map/ppermute | solution.py:21
  46.1 29.9 %collective-permute-done.1 = bf16[256,512]{0,1:T(8,128)(2,1)} collective-permute-done((bf16[256,512]{0,1:T(8,128)(2,1)S(1)}, bf16[256,512]{0,1:T(8,128)(2,1)}, u32[]{:S(2)}, u32[]{:S(2)}) %collective-permute-start.1) | collective-permute-done | bytes 262176 | tf_op jit(solution)/shard_map/ppermute | solution.py:29
  77.0 8.8 %collective-permute-start.4 = (bf16[256,256]{0,1:T(8,128)(2,1)S(1)}, bf16[256,256]{0,1:T(8,128)(2,1)S(1)}, u32[]{:S(2)}, u32[]{:S(2)}) collective-permute-start(bf16[256,256]{0,1:T(8,128)(2,1)S(1)} %slice.150), channel_id=1, source_target_pairs={{0,12},{1,13},{2,14},{3,15},{4,0},{5,1},{6,2},{7,3},{8,4},{9,5},{1... | collective-permute-start | bytes 393224 | tf_op jit(solution)/shard_map/ppermute | solution.py:29
  86.7 1.9 %collective-permute-start.5 = (bf16[256,256]{0,1:T(8,128)(2,1)S(1)}, bf16[256,256]{0,1:T(8,128)(2,1)S(1)}, u32[]{:S(2)}, u32[]{:S(2)}) collective-permute-start(bf16[256,256]{0,1:T(8,128)(2,1)S(1)} %slice.151), channel_id=1, source_target_pairs={{0,4},{1,5},{2,6},{3,7},{4,8},{5,9},{6,10},{7,11},{8,12},{9,13},{1... | collective-permute-start | bytes 393224 | tf_op jit(solution)/shard_map/ppermute | solution.py:29
  88.6 7.8 %collective-permute-start.14 = (bf16[256,256]{0,1:T(8,128)(2,1)S(1)}, bf16[256,256]{0,1:T(8,128)(2,1)S(1)}, u32[]{:S(2)}, u32[]{:S(2)}) collective-permute-start(bf16[256,256]{0,1:T(8,128)(2,1)S(1)} %slice.165), channel_id=1, source_target_pairs={{0,12},{1,13},{2,14},{3,15},{4,0},{5,1},{6,2},{7,3},{8,4},{9,5},{1... | collective-permute-start | bytes 393224 | tf_op jit(solution)/shard_map/ppermute | solution.py:29
  96.5 1.9 %collective-permute-start.15 = (bf16[256,256]{0,1:T(8,128)(2,1)S(1)}, bf16[256,256]{0,1:T(8,128)(2,1)S(1)}, u32[]{:S(2)}, u32[]{:S(2)}) collective-permute-start(bf16[256,256]{0,1:T(8,128)(2,1)S(1)} %slice.166), channel_id=1, source_target_pairs={{0,4},{1,5},{2,6},{3,7},{4,8},{5,9},{6,10},{7,11},{8,12},{9,13},{1... | collective-permute-start | bytes 393224 | tf_op jit(solution)/shard_map/ppermute | solution.py:29
  98.4 10.9 %collective-permute-done.3 = bf16[256,512]{1,0:T(8,128)(2,1)S(1)} collective-permute-done((bf16[256,512]{1,0:T(8,128)(2,1)S(1)}, bf16[256,512]{1,0:T(8,128)(2,1)S(1)}, u32[]{:S(2)}, u32[]{:S(2)}) %collective-permute-start.3) | collective-permute-done | bytes 262176 | tf_op jit(solution)/shard_map/ppermute | solution.py:21
  114.7 2.4 %collective-permute-start.16 = (bf16[256,512]{0,1:T(8,128)(2,1)S(1)}, bf16[256,512]{0,1:T(8,128)(2,1)S(1)}, u32[]{:S(2)}, u32[]{:S(2)}) collective-permute-start(bf16[256,512]{0,1:T(8,128)(2,1)S(1)} %fusion.20), channel_id=1, source_target_pairs={{0,2},{1,3},{2,0},{3,1},{4,6},{5,7},{6,4},{7,5},{8,10},{9,11},{10,... | collective-permute-start | bytes 786440 | tf_op jit(solution)/shard_map/ppermute | solution.py:21
  117.6 4.3 %collective-permute-start.6 = (bf16[256,512]{0,1:T(8,128)(2,1)S(1)}, bf16[256,512]{0,1:T(8,128)(2,1)S(1)}, u32[]{:S(2)}, u32[]{:S(2)}) collective-permute-start(bf16[256,512]{0,1:T(8,128)(2,1)S(1)} %fusion.26), channel_id=1, source_target_pairs={{0,2},{1,3},{2,0},{3,1},{4,6},{5,7},{6,4},{7,5},{8,10},{9,11},{10,... | collective-permute-start | bytes 786440 | tf_op jit(solution)/shard_map/ppermute | solution.py:21
  122.0 15.6 %collective-permute-done.16 = bf16[256,512]{0,1:T(8,128)(2,1)S(1)} collective-permute-done((bf16[256,512]{0,1:T(8,128)(2,1)S(1)}, bf16[256,512]{0,1:T(8,128)(2,1)S(1)}, u32[]{:S(2)}, u32[]{:S(2)}) %collective-permute-start.16) | collective-permute-done | bytes 262176 | tf_op jit(solution)/shard_map/ppermute | solution.py:21
  138.1 1.9 %collective-permute-start.17 = (bf16[256,512]{0,1:T(8,128)(2,1)S(1)}, bf16[256,512]{0,1:T(8,128)(2,1)S(1)}, u32[]{:S(2)}, u32[]{:S(2)}) collective-permute-start(bf16[256,512]{0,1:T(8,128)(2,1)S(1)} %fusion.19), channel_id=1, source_target_pairs={{0,1},{1,0},{2,3},{3,2},{4,5},{5,4},{6,7},{7,6},{8,9},{9,8},{10,11... | collective-permute-start | bytes 786440 | tf_op jit(solution)/shard_map/ppermute | solution.py:21
  141.8 2.7 %collective-permute-start.7 = (bf16[256,512]{0,1:T(8,128)(2,1)S(1)}, bf16[256,512]{0,1:T(8,128)(2,1)S(1)}, u32[]{:S(2)}, u32[]{:S(2)}) collective-permute-start(bf16[256,512]{0,1:T(8,128)(2,1)S(1)} %fusion.25), channel_id=1, source_target_pairs={{0,1},{1,0},{2,3},{3,2},{4,5},{5,4},{6,7},{7,6},{8,9},{9,8},{10,11... | collective-permute-start | bytes 786440 | tf_op jit(solution)/shard_map/ppermute | solution.py:21
  144.5 4.7 %collective-permute-done.17 = bf16[256,512]{0,1:T(8,128)(2,1)S(1)} collective-permute-done((bf16[256,512]{0,1:T(8,128)(2,1)S(1)}, bf16[256,512]{0,1:T(8,128)(2,1)S(1)}, u32[]{:S(2)}, u32[]{:S(2)}) %collective-permute-start.17) | collective-permute-done | bytes 262176 | tf_op jit(solution)/shard_map/ppermute | solution.py:21
  149.7 2.3 %collective-permute-start.18 = (bf16[256,512]{0,1:T(8,128)(2,1)S(1)}, bf16[256,512]{0,1:T(8,128)(2,1)S(1)}, u32[]{:S(2)}, u32[]{:S(2)}) collective-permute-start(bf16[256,512]{0,1:T(8,128)(2,1)S(1)} %fusion.18), channel_id=1, source_target_pairs={{0,256},{32,288},{64,320},{96,352},{128,384},{160,416},{192,448},{... | collective-permute-start | bytes 786440 | tf_op jit(solution)/shard_map/ppermute | solution.py:21
  153.0 3.2 %collective-permute-start.8 = (bf16[256,512]{0,1:T(8,128)(2,1)S(1)}, bf16[256,512]{0,1:T(8,128)(2,1)S(1)}, u32[]{:S(2)}, u32[]{:S(2)}) collective-permute-start(bf16[256,512]{0,1:T(8,128)(2,1)S(1)} %fusion.24), channel_id=1, source_target_pairs={{0,256},{32,288},{64,320},{96,352},{128,384},{160,416},{192,448},{... | collective-permute-start | bytes 786440 | tf_op jit(solution)/shard_map/ppermute | solution.py:21
  156.2 4.6 %collective-permute-done.18 = bf16[256,512]{0,1:T(8,128)(2,1)S(1)} collective-permute-done((bf16[256,512]{0,1:T(8,128)(2,1)S(1)}, bf16[256,512]{0,1:T(8,128)(2,1)S(1)}, u32[]{:S(2)}, u32[]{:S(2)}) %collective-permute-start.18) | collective-permute-done | bytes 262176 | tf_op jit(solution)/shard_map/ppermute | solution.py:21
  161.3 2.4 %collective-permute-start.19 = (bf16[256,512]{0,1:T(8,128)(2,1)S(1)}, bf16[256,512]{0,1:T(8,128)(2,1)S(1)}, u32[]{:S(2)}, u32[]{:S(2)}) collective-permute-start(bf16[256,512]{0,1:T(8,128)(2,1)S(1)} %fusion.17), channel_id=1, source_target_pairs={{0,128},{32,160},{64,192},{96,224},{128,0},{160,32},{192,64},{224,... | collective-permute-start | bytes 786440 | tf_op jit(solution)/shard_map/ppermute | solution.py:21
  164.2 5.0 %collective-permute-start.9 = (bf16[256,512]{0,1:T(8,128)(2,1)S(1)}, bf16[256,512]{0,1:T(8,128)(2,1)S(1)}, u32[]{:S(2)}, u32[]{:S(2)}) collective-permute-start(bf16[256,512]{0,1:T(8,128)(2,1)S(1)} %fusion.23), channel_id=1, source_target_pairs={{0,128},{32,160},{64,192},{96,224},{128,0},{160,32},{192,64},{224,... | collective-permute-start | bytes 786440 | tf_op jit(solution)/shard_map/ppermute | solution.py:21
  169.2 4.7 %collective-permute-done.19 = bf16[256,512]{0,1:T(8,128)(2,1)S(1)} collective-permute-done((bf16[256,512]{0,1:T(8,128)(2,1)S(1)}, bf16[256,512]{0,1:T(8,128)(2,1)S(1)}, u32[]{:S(2)}, u32[]{:S(2)}) %collective-permute-start.19) | collective-permute-done | bytes 262176 | tf_op jit(solution)/shard_map/ppermute | solution.py:21
  174.5 2.9 %collective-permute-start.20 = (bf16[256,512]{1,0:T(8,128)(2,1)S(1)}, bf16[256,512]{1,0:T(8,128)(2,1)S(1)}, u32[]{:S(2)}, u32[]{:S(2)}) collective-permute-start(bf16[256,512]{1,0:T(8,128)(2,1)S(1)} %fusion.16.own_ref), channel_id=1, source_target_pairs={{0,64},{32,96},{64,0},{96,32},{128,192},{160,224},{192,128},{224,1... | collective-permute-start | bytes 786440 | tf_op jit(solution)/shard_map/ppermute | solution.py:21
  177.4 2.2 %collective-permute-done.9 = bf16[256,512]{0,1:T(8,128)(2,1)S(1)} collective-permute-done((bf16[256,512]{0,1:T(8,128)(2,1)S(1)}, bf16[256,512]{0,1:T(8,128)(2,1)S(1)}, u32[]{:S(2)}, u32[]{:S(2)}) %collective-permute-start.9) | collective-permute-done | bytes 262176 | tf_op jit(solution)/shard_map/ppermute | solution.py:21
  180.1 2.9 %collective-permute-start.10 = (bf16[256,512]{1,0:T(8,128)(2,1)S(1)}, bf16[256,512]{1,0:T(8,128)(2,1)S(1)}, u32[]{:S(2)}, u32[]{:S(2)}) collective-permute-start(bf16[256,512]{1,0:T(8,128)(2,1)S(1)} %fusion.22.own_ref), channel_id=1, source_target_pairs={{0,64},{32,96},{64,0},{96,32},{128,192},{160,224},{192,128},{224,1... | collective-permute-start | bytes 786440 | tf_op jit(solution)/shard_map/ppermute | solution.py:21
  183.3 1.6 shard_map.46.refs_0_
  184.9 3.5 %collective-permute-done.10.other_ref = bf16[256,512]{1,0:T(8,128)(2,1)S(1)} collective-permute-done((bf16[256,512]{1,0:T(8,128)(2,1)S(1)}, bf16[256,512]{1,0:T(8,128)(2,1)S(1)}, u32[]{:S(2)}, u32[]{:S(2)}) %collective-permute-start.10) | collective-permute-done | bytes 262176 | tf_op jit(solution)/shard_map/ppermute | solution.py:21
  (59 shorter events, 18.9 us)
Async XLA Ops:
  0.0 0.9 copy-start
  2.5 12.6 %collective-permute-start = (bf16[256,512]{1,0:T(8,128)(2,1)S(1)}, bf16[256,512]{1,0:T(8,128)(2,1)S(1)}, u32[]{:S(2)}, u32[]{:S(2)}) collective-permute-start(bf16[256,512]{1,0:T(8,128)(2,1)S(1)} %get-tuple-element.14), channel_id=1, source_target_pairs={{0,16},{1,17},{2,18},{3,19},{4,20},{5,21},{6,22},{7,23},{8,24},{9,... | collective-permute-start | bytes 786440 | tf_op jit(solution)/shard_map/ppermute | solution.py:21
  6.7 23.6 %collective-permute-start.11 = (bf16[256,512]{1,0:T(8,128)(2,1)S(1)}, bf16[256,512]{1,0:T(8,128)(2,1)S(1)}, u32[]{:S(2)}, u32[]{:S(2)}) collective-permute-start(bf16[256,512]{1,0:T(8,128)(2,1)S(1)} %get-tuple-element.13), channel_id=1, source_target_pairs={{0,16},{1,17},{2,18},{3,19},{4,20},{5,21},{6,22},{7,23},{8,24},{9,... | collective-permute-start | bytes 786440 | tf_op jit(solution)/shard_map/ppermute | solution.py:21
  15.6 60.4 %collective-permute-start.1 = (bf16[256,512]{0,1:T(8,128)(2,1)S(1)}, bf16[256,512]{0,1:T(8,128)(2,1)}, u32[]{:S(2)}, u32[]{:S(2)}) collective-permute-start(bf16[256,512]{0,1:T(8,128)(2,1)S(1)} %fusion.27), channel_id=1, source_target_pairs={{0,12},{1,13},{2,14},{3,15},{4,0},{5,1},{6,2},{7,3},{8,4},{9,5},{1... | collective-permute-start | bytes 786440 | tf_op jit(solution)/shard_map/ppermute | solution.py:29
  28.4 57.4 %collective-permute-start.2 = (bf16[256,512]{0,1:T(8,128)(2,1)S(1)}, bf16[256,512]{0,1:T(8,128)(2,1)}, u32[]{:S(2)}, u32[]{:S(2)}) collective-permute-start(bf16[256,512]{0,1:T(8,128)(2,1)S(1)} %fusion.27), channel_id=1, source_target_pairs={{0,4},{1,5},{2,6},{3,7},{4,8},{5,9},{6,10},{7,11},{8,12},{9,13},{1... | collective-permute-start | bytes 786440 | tf_op jit(solution)/shard_map/ppermute | solution.py:29
  30.9 57.7 %collective-permute-start.12 = (bf16[256,512]{0,1:T(8,128)(2,1)S(1)}, bf16[256,512]{0,1:T(8,128)(2,1)S(1)}, u32[]{:S(2)}, u32[]{:S(2)}) collective-permute-start(bf16[256,512]{0,1:T(8,128)(2,1)S(1)} %fusion.21), channel_id=1, source_target_pairs={{0,12},{1,13},{2,14},{3,15},{4,0},{5,1},{6,2},{7,3},{8,4},{9,5},{1... | collective-permute-start | bytes 786440 | tf_op jit(solution)/shard_map/ppermute | solution.py:29
  38.7 57.7 %collective-permute-start.13 = (bf16[256,512]{0,1:T(8,128)(2,1)S(1)}, bf16[256,512]{0,1:T(8,128)(2,1)S(1)}, u32[]{:S(2)}, u32[]{:S(2)}) collective-permute-start(bf16[256,512]{0,1:T(8,128)(2,1)S(1)} %fusion.21), channel_id=1, source_target_pairs={{0,4},{1,5},{2,6},{3,7},{4,8},{5,9},{6,10},{7,11},{8,12},{9,13},{1... | collective-permute-start | bytes 786440 | tf_op jit(solution)/shard_map/ppermute | solution.py:29
  40.7 68.7 %collective-permute-start.3 = (bf16[256,512]{1,0:T(8,128)(2,1)S(1)}, bf16[256,512]{1,0:T(8,128)(2,1)S(1)}, u32[]{:S(2)}, u32[]{:S(2)}) collective-permute-start(bf16[256,512]{1,0:T(8,128)(2,1)S(1)} %get-tuple-element.9), channel_id=1, source_target_pairs={{0,4},{1,5},{2,6},{3,7},{4,0},{5,1},{6,2},{7,3},{8,12},{9,13},{10,... | collective-permute-start | bytes 786440 | tf_op jit(solution)/shard_map/ppermute | solution.py:21
  77.0 35.5 %collective-permute-start.4 = (bf16[256,256]{0,1:T(8,128)(2,1)S(1)}, bf16[256,256]{0,1:T(8,128)(2,1)S(1)}, u32[]{:S(2)}, u32[]{:S(2)}) collective-permute-start(bf16[256,256]{0,1:T(8,128)(2,1)S(1)} %slice.150), channel_id=1, source_target_pairs={{0,12},{1,13},{2,14},{3,15},{4,0},{5,1},{6,2},{7,3},{8,4},{9,5},{1... | collective-permute-start | bytes 393224 | tf_op jit(solution)/shard_map/ppermute | solution.py:29
  86.7 25.8 %collective-permute-start.5 = (bf16[256,256]{0,1:T(8,128)(2,1)S(1)}, bf16[256,256]{0,1:T(8,128)(2,1)S(1)}, u32[]{:S(2)}, u32[]{:S(2)}) collective-permute-start(bf16[256,256]{0,1:T(8,128)(2,1)S(1)} %slice.151), channel_id=1, source_target_pairs={{0,4},{1,5},{2,6},{3,7},{4,8},{5,9},{6,10},{7,11},{8,12},{9,13},{1... | collective-permute-start | bytes 393224 | tf_op jit(solution)/shard_map/ppermute | solution.py:29
  88.6 24.9 %collective-permute-start.14 = (bf16[256,256]{0,1:T(8,128)(2,1)S(1)}, bf16[256,256]{0,1:T(8,128)(2,1)S(1)}, u32[]{:S(2)}, u32[]{:S(2)}) collective-permute-start(bf16[256,256]{0,1:T(8,128)(2,1)S(1)} %slice.165), channel_id=1, source_target_pairs={{0,12},{1,13},{2,14},{3,15},{4,0},{5,1},{6,2},{7,3},{8,4},{9,5},{1... | collective-permute-start | bytes 393224 | tf_op jit(solution)/shard_map/ppermute | solution.py:29
  96.5 17.1 %collective-permute-start.15 = (bf16[256,256]{0,1:T(8,128)(2,1)S(1)}, bf16[256,256]{0,1:T(8,128)(2,1)S(1)}, u32[]{:S(2)}, u32[]{:S(2)}) collective-permute-start(bf16[256,256]{0,1:T(8,128)(2,1)S(1)} %slice.166), channel_id=1, source_target_pairs={{0,4},{1,5},{2,6},{3,7},{4,8},{5,9},{6,10},{7,11},{8,12},{9,13},{1... | collective-permute-start | bytes 393224 | tf_op jit(solution)/shard_map/ppermute | solution.py:29
  114.7 22.9 %collective-permute-start.16 = (bf16[256,512]{0,1:T(8,128)(2,1)S(1)}, bf16[256,512]{0,1:T(8,128)(2,1)S(1)}, u32[]{:S(2)}, u32[]{:S(2)}) collective-permute-start(bf16[256,512]{0,1:T(8,128)(2,1)S(1)} %fusion.20), channel_id=1, source_target_pairs={{0,2},{1,3},{2,0},{3,1},{4,6},{5,7},{6,4},{7,5},{8,10},{9,11},{10,... | collective-permute-start | bytes 786440 | tf_op jit(solution)/shard_map/ppermute | solution.py:21
  117.6 23.6 %collective-permute-start.6 = (bf16[256,512]{0,1:T(8,128)(2,1)S(1)}, bf16[256,512]{0,1:T(8,128)(2,1)S(1)}, u32[]{:S(2)}, u32[]{:S(2)}) collective-permute-start(bf16[256,512]{0,1:T(8,128)(2,1)S(1)} %fusion.26), channel_id=1, source_target_pairs={{0,2},{1,3},{2,0},{3,1},{4,6},{5,7},{6,4},{7,5},{8,10},{9,11},{10,... | collective-permute-start | bytes 786440 | tf_op jit(solution)/shard_map/ppermute | solution.py:21
  138.1 11.1 %collective-permute-start.17 = (bf16[256,512]{0,1:T(8,128)(2,1)S(1)}, bf16[256,512]{0,1:T(8,128)(2,1)S(1)}, u32[]{:S(2)}, u32[]{:S(2)}) collective-permute-start(bf16[256,512]{0,1:T(8,128)(2,1)S(1)} %fusion.19), channel_id=1, source_target_pairs={{0,1},{1,0},{2,3},{3,2},{4,5},{5,4},{6,7},{7,6},{8,9},{9,8},{10,11... | collective-permute-start | bytes 786440 | tf_op jit(solution)/shard_map/ppermute | solution.py:21
  141.8 10.6 %collective-permute-start.7 = (bf16[256,512]{0,1:T(8,128)(2,1)S(1)}, bf16[256,512]{0,1:T(8,128)(2,1)S(1)}, u32[]{:S(2)}, u32[]{:S(2)}) collective-permute-start(bf16[256,512]{0,1:T(8,128)(2,1)S(1)} %fusion.25), channel_id=1, source_target_pairs={{0,1},{1,0},{2,3},{3,2},{4,5},{5,4},{6,7},{7,6},{8,9},{9,8},{10,11... | collective-permute-start | bytes 786440 | tf_op jit(solution)/shard_map/ppermute | solution.py:21
  149.7 11.1 %collective-permute-start.18 = (bf16[256,512]{0,1:T(8,128)(2,1)S(1)}, bf16[256,512]{0,1:T(8,128)(2,1)S(1)}, u32[]{:S(2)}, u32[]{:S(2)}) collective-permute-start(bf16[256,512]{0,1:T(8,128)(2,1)S(1)} %fusion.18), channel_id=1, source_target_pairs={{0,256},{32,288},{64,320},{96,352},{128,384},{160,416},{192,448},{... | collective-permute-start | bytes 786440 | tf_op jit(solution)/shard_map/ppermute | solution.py:21
  153.0 10.7 %collective-permute-start.8 = (bf16[256,512]{0,1:T(8,128)(2,1)S(1)}, bf16[256,512]{0,1:T(8,128)(2,1)S(1)}, u32[]{:S(2)}, u32[]{:S(2)}) collective-permute-start(bf16[256,512]{0,1:T(8,128)(2,1)S(1)} %fusion.24), channel_id=1, source_target_pairs={{0,256},{32,288},{64,320},{96,352},{128,384},{160,416},{192,448},{... | collective-permute-start | bytes 786440 | tf_op jit(solution)/shard_map/ppermute | solution.py:21
  161.3 12.6 %collective-permute-start.19 = (bf16[256,512]{0,1:T(8,128)(2,1)S(1)}, bf16[256,512]{0,1:T(8,128)(2,1)S(1)}, u32[]{:S(2)}, u32[]{:S(2)}) collective-permute-start(bf16[256,512]{0,1:T(8,128)(2,1)S(1)} %fusion.17), channel_id=1, source_target_pairs={{0,128},{32,160},{64,192},{96,224},{128,0},{160,32},{192,64},{224,... | collective-permute-start | bytes 786440 | tf_op jit(solution)/shard_map/ppermute | solution.py:21
  164.2 15.3 %collective-permute-start.9 = (bf16[256,512]{0,1:T(8,128)(2,1)S(1)}, bf16[256,512]{0,1:T(8,128)(2,1)S(1)}, u32[]{:S(2)}, u32[]{:S(2)}) collective-permute-start(bf16[256,512]{0,1:T(8,128)(2,1)S(1)} %fusion.23), channel_id=1, source_target_pairs={{0,128},{32,160},{64,192},{96,224},{128,0},{160,32},{192,64},{224,... | collective-permute-start | bytes 786440 | tf_op jit(solution)/shard_map/ppermute | solution.py:21
  174.2 9.1 %copy-start.1 = (bf16[1,1,256,256]{3,2,1,0:T(8,128)(2,1)S(1)}, bf16[1,1,256,256]{3,2,1,0:T(8,128)(2,1)}, u32[]{:S(2)}) copy-start(bf16[1,1,256,256]{3,2,1,0:T(8,128)(2,1)} %param.7) | copy-start | bytes 393220
  174.5 8.8 %collective-permute-start.20 = (bf16[256,512]{1,0:T(8,128)(2,1)S(1)}, bf16[256,512]{1,0:T(8,128)(2,1)S(1)}, u32[]{:S(2)}, u32[]{:S(2)}) collective-permute-start(bf16[256,512]{1,0:T(8,128)(2,1)S(1)} %fusion.16.own_ref), channel_id=1, source_target_pairs={{0,64},{32,96},{64,0},{96,32},{128,192},{160,224},{192,128},{224,1... | collective-permute-start | bytes 786440 | tf_op jit(solution)/shard_map/ppermute | solution.py:21
  180.1 8.3 %collective-permute-start.10 = (bf16[256,512]{1,0:T(8,128)(2,1)S(1)}, bf16[256,512]{1,0:T(8,128)(2,1)S(1)}, u32[]{:S(2)}, u32[]{:S(2)}) collective-permute-start(bf16[256,512]{1,0:T(8,128)(2,1)S(1)} %fusion.22.own_ref), channel_id=1, source_target_pairs={{0,64},{32,96},{64,0},{96,32},{128,192},{160,224},{192,128},{224,1... | collective-permute-start | bytes 786440 | tf_op jit(solution)/shard_map/ppermute | solution.py:21
